TPU v7x, 32 devices: a whole 2x2x4 slice. The times are simulated.
32 devices in a mesh: row: 8 (over y, x, core), col: 4 (over z).
Axes of the slice: x: 2, y: 2, z: 4, core: 2. Of those that a mesh axis runs over, the one named last changes fastest.
Arguments:
- alignment_state: bfloat16 [128, 128, 256], P('col', 'row'), may hold values from -6 to 6
- layer_norm_gain: float32 [256], replicated, may hold values from 0.1 to 1.9
- left_weight_matrix: bfloat16 [256, 32], replicated, may hold values from -0.375 to 0.375
- right_weight_matrix: bfloat16 [256, 32], replicated, may hold values from -0.375 to 0.375
- output_weight_matrix: bfloat16 [1024, 128], replicated, may hold values from -0.1875 to 0.1875
- output_bias_vector: float32 [128], replicated, may hold values from -3 to 3
- pair_update_cotangent: bfloat16 [128, 128, 128], P('row', 'col'), may hold values from -40 to 40
Outputs:
- pair_update_output: bfloat16 [128, 128, 128], P('row', 'col')
- alignment_gradient: bfloat16 [128, 128, 256], P('col', 'row')
- left_weight_gradient: float32 [256, 32], replicated
- right_weight_gradient: float32 [256, 32], replicated
- out_w_grad: float32 [1024, 128], P(('row', 'col'))
- norm_gain_gradient: float32 [256], replicated
- output_bias_gradient: float32 [128], replicated
All inputs are finite; a program needn't handle non-finite values.
Results may differ from a plain program's by a relative error of at most 0.024.
Values may be sent and summed in bfloat16 or wider, within the bound.
No kernel may reach another device: no remote copies, remote signals or barrier semaphores. Data moves between devices by JAX's collectives and lax.ppermute only.
A program may use at most 64 MiB of HBM per device.

v0:
```python
import jax
import jax.numpy as jnp
from jax import lax
from jax.sharding import PartitionSpec as P


def from_root(block, axis, holder):
    block = jnp.where(lax.axis_index(axis) == holder, block, jnp.zeros_like(block))
    return lax.psum(block, axis)


def apply_layer_norm(alignment_state):
    value_entries = alignment_state.astype(jnp.float32)
    center = value_entries - jnp.mean(value_entries, axis=-1, keepdims=True)
    inverse_deviation = lax.rsqrt(jnp.mean(center * center, axis=-1, keepdims=True) + 1e-05)
    return (center * inverse_deviation, inverse_deviation)


def on_device(
    alignment_state,
    layer_norm_gain,
    left_weight_matrix,
    right_weight_matrix,
    output_weight_matrix,
    output_bias_vector,
    pair_update_cotangent,
):
    sequence_block_local, residue_block_local, alignment_weight = alignment_state.shape
    proj_w = left_weight_matrix.shape[1]
    pair_w = output_weight_matrix.shape[1]
    row_count = lax.axis_size("row")
    col_count = lax.axis_size("col")
    row_ratio = row_count // col_count
    total_res = residue_block_local * row_count
    col_res = residue_block_local * row_ratio
    col_index = lax.axis_index("col")
    row_index = lax.axis_index("row")
    normed_alignment, inverse_deviation = apply_layer_norm(alignment_state)
    layer_norm_output = (normed_alignment * layer_norm_gain).astype(jnp.bfloat16)
    normed_flat_rows = layer_norm_output.reshape(-1, alignment_weight)
    left_local = (
        jnp.dot(normed_flat_rows, left_weight_matrix, preferred_element_type=jnp.float32)
        .astype(jnp.bfloat16)
        .reshape(sequence_block_local, residue_block_local, proj_w)
    )
    right_local = (
        jnp.dot(normed_flat_rows, right_weight_matrix, preferred_element_type=jnp.float32)
        .astype(jnp.bfloat16)
        .reshape(sequence_block_local, residue_block_local, proj_w)
    )
    left_all, right_rows = (
        lax.all_gather(left_local, "col", axis=0, tiled=True),
        lax.all_gather(right_local, "col", axis=0, tiled=True),
    )
    seq_total = left_all.shape[0]
    right_every = lax.all_gather(right_rows, "row", axis=1, tiled=True)
    right_block = lax.dynamic_slice_in_dim(right_every, col_index * col_res, col_res, 1)
    block_res = min(8, residue_block_local)

    def visit(totals, row_start):
        right_acc, projection_running_sum = totals
        left_part = lax.dynamic_slice_in_dim(left_all, row_start, block_res, 1)
        cot_part = lax.dynamic_slice_in_dim(pair_update_cotangent, row_start, block_res, 0)
        outer_prod = jnp.einsum(
            "sic,sjd->ijcd", left_part, right_block, preferred_element_type=jnp.float32
        )
        outer_flat = (
            (outer_prod / seq_total)
            .astype(jnp.bfloat16)
            .reshape(block_res * col_res, proj_w * proj_w)
        )
        cot_flat = cot_part.reshape(block_res * col_res, pair_w)
        pair_part = (
            jnp.dot(outer_flat, output_weight_matrix, preferred_element_type=jnp.float32)
            + output_bias_vector
        ).astype(jnp.bfloat16)
        projection_running_sum = projection_running_sum + lax.dot_general(
            outer_flat, cot_flat, (((0,), (0,)), ((), ())), preferred_element_type=jnp.float32
        )
        outer_grad = lax.dot_general(
            cot_flat,
            output_weight_matrix,
            (((1,), (1,)), ((), ())),
            preferred_element_type=jnp.float32,
        ).astype(jnp.bfloat16)
        outer_grad = outer_grad.reshape(block_res, col_res, proj_w, proj_w)
        left_part_grad = (
            jnp.einsum("ijcd,sjd->sic", outer_grad, right_block, preferred_element_type=jnp.float32)
            / seq_total
        )
        right_acc = (
            right_acc
            + jnp.einsum("ijcd,sic->sjd", outer_grad, left_part, preferred_element_type=jnp.float32)
            / seq_total
        )
        return (
            (right_acc, projection_running_sum),
            (pair_part.reshape(block_res, col_res, pair_w), left_part_grad),
        )

    starts = jnp.arange(residue_block_local // block_res, dtype=jnp.int32) * block_res
    initial = (
        jnp.zeros((seq_total, col_res, proj_w), jnp.float32),
        jnp.zeros((proj_w * proj_w, pair_w), jnp.float32),
    )
    (right_acc, projection_running_sum), (pair_parts, left_parts) = lax.scan(visit, initial, starts)
    pair_update_output = pair_parts.reshape(residue_block_local, col_res, pair_w)
    left_partial = jnp.transpose(left_parts, (1, 0, 2, 3)).reshape(
        seq_total, residue_block_local, proj_w
    )
    left_d = lax.psum_scatter(
        left_partial.astype(jnp.bfloat16), "col", scatter_dimension=0, tiled=True
    )
    right_full = lax.psum(right_acc.astype(jnp.bfloat16), "row").astype(jnp.float32)
    right_half = lax.dynamic_slice_in_dim(
        right_full, row_index % row_ratio * residue_block_local, residue_block_local, 1
    )
    right_home = from_root(right_half.astype(jnp.bfloat16), "col", row_index // row_ratio).astype(
        right_half.dtype
    )
    right_d = lax.dynamic_slice_in_dim(
        right_home, col_index * sequence_block_local, sequence_block_local, 0
    ).astype(jnp.bfloat16)
    left_flat = left_d.reshape(-1, proj_w)
    right_flat = right_d.reshape(-1, proj_w)
    normed_derivative = lax.dot_general(
        left_flat, left_weight_matrix, (((1,), (1,)), ((), ())), preferred_element_type=jnp.float32
    )
    normed_derivative = normed_derivative + lax.dot_general(
        right_flat,
        right_weight_matrix,
        (((1,), (1,)), ((), ())),
        preferred_element_type=jnp.float32,
    )
    normed_derivative = normed_derivative.reshape(
        sequence_block_local, residue_block_local, alignment_weight
    )
    scaled_product = normed_derivative * layer_norm_gain
    alignment_gradient = (
        (
            scaled_product
            - jnp.mean(scaled_product, axis=-1, keepdims=True)
            - normed_alignment * jnp.mean(scaled_product * normed_alignment, axis=-1, keepdims=True)
        )
        * inverse_deviation
    ).astype(jnp.bfloat16)
    weight_left = lax.dot_general(
        normed_flat_rows, left_flat, (((0,), (0,)), ((), ())), preferred_element_type=jnp.float32
    )
    weight_right = lax.dot_general(
        normed_flat_rows, right_flat, (((0,), (0,)), ((), ())), preferred_element_type=jnp.float32
    )
    gain_part = jnp.sum(normed_derivative * normed_alignment, axis=(0, 1))
    bias_part = jnp.sum(pair_update_cotangent, axis=(0, 1), dtype=jnp.float32)
    param_totals = lax.psum((weight_left, weight_right, gain_part, bias_part), ("row", "col"))
    proj_partial = lax.psum_scatter(
        projection_running_sum.astype(jnp.bfloat16), "row", scatter_dimension=0, tiled=True
    ).astype(jnp.float32)
    proj_total = lax.psum_scatter(proj_partial, "col", scatter_dimension=0, tiled=True)
    return (
        pair_update_output,
        alignment_gradient,
        param_totals[0] / total_res,
        param_totals[1] / total_res,
        proj_total / total_res,
        param_totals[2] / total_res,
        param_totals[3] / total_res,
    )


def solution(mesh):
    return jax.shard_map(
        on_device,
        mesh=mesh,
        in_specs=(P("col", "row", None), P(), P(), P(), P(), P(), P("row", "col", None)),
        out_specs=(
            P("row", "col", None),
            P("col", "row", None),
            P(),
            P(),
            P(("row", "col"), None),
            P(),
            P(),
        ),
        check_vma=False,
    )
```

profile of v0, /device:TPU:0, one launch (start us, length us, event | category | flops | bytes accessed | tf_op | source)
XLA Modules:
  0.0 416.1 jit_solution(7871246451103388164)
XLA Ops:
  7.2 1.1 convert_reduce_fusion
  8.4 1.2 fusion.27
  9.6 1.2 fusion.21
  10.8 0.2 convolution_convert_fusion.1
  11.0 0.1 copy.42
  11.1 18.0 %all_gather.10 = bf16[128,16,32]{2,1,0:T(8,128)(2,1)} all-gather(bf16[32,16,32]{2,1,0:T(8,128)(2,1)S(1)} %bitcast.126), channel_id=1, replica_groups=mesh['row'=8,'col'=4] {'col'}, dimensions={0}, use_global_device_ids=true | all-gather | bytes 163840 | tf_op jit(solution)/shard_map/all_gather | solution.py:53
  29.2 0.2 convolution_convert_fusion.2
  29.4 0.1 copy.41
  29.6 16.3 %all_gather.9 = bf16[128,16,32]{2,1,0:T(8,128)(2,1)S(1)} all-gather(bf16[32,16,32]{2,1,0:T(8,128)(2,1)S(1)} %bitcast.127), channel_id=1, replica_groups=mesh['row'=8,'col'=4] {'col'}, dimensions={0}, use_global_device_ids=true | all-gather | bytes 163840 | tf_op jit(solution)/shard_map/all_gather | solution.py:52
  45.9 0.4 copy.43
  46.3 0.5 iota_multiply_fusion
  46.8 21.7 %all-gather.2.cloned.1.call-done = bf16[128,128,32]{2,1,0:T(8,128)(2,1)} async-done(((bf16[128,16,32]{2,1,0:T(8,128)(2,1)}), bf16[128,128,32]{2,1,0:T(8,128)(2,1)}) %all-gather.2.cloned.1.call-update) | async-done | bytes 1048592 | tf_op jit(solution)/shard_map/all_gather | solution.py:56
  68.5 1.3 constant_dynamic-slice_fusion.1
  69.8 1.8 copy.44
  71.6 32.6 %while.17 = (s32[]{:T(128)}, f32[128,32,32]{0,2,1:T(8,128)}, f32[1024,128]{1,0:T(8,128)S(1)}, bf16[2,8,32,128]{3,2,1,0:T(8,128)(2,1)}, bf16[2,128,8,32]{1,3,2,0:...) while((s32[]{:T(128)}, f32[128,32,32]{0,2,1:T(8,128)}, ...), condition=%wide.region_3.4_spmd.clone, body=%wide.region_2.3_spmd.clone.sunk | while | flops 404193280 | bytes 15928666 | solution.py:106
  71.6 1.2 dynamic_slice.46
  74.8 1.7 fusion.79
  76.5 2.2 reshape.95
  78.7 0.9 constant_dynamic-slice_fusion.3
  79.5 0.5 convolution_add_fusion.4
  80.0 0.8 copy-done.2
  80.8 0.3 convolution_convert_fusion.4
  81.1 1.6 reshape.94
  82.7 1.5 fusion.78
  84.3 0.3 fusion.80
  84.6 0.6 copy-done.17
  85.3 2.1 fusion.81
  87.4 1.2 dynamic_slice.46
  90.6 1.7 fusion.79
  92.2 2.2 reshape.95
  94.5 0.9 constant_dynamic-slice_fusion.3
  95.3 0.5 convolution_add_fusion.4
  95.8 0.8 copy-done.2
  96.6 0.3 convolution_convert_fusion.4
  96.9 1.6 reshape.94
  98.5 2.6 fusion.78
  101.1 0.3 fusion.80
  101.5 0.6 copy-done.17
  102.1 2.1 fusion.81
  104.3 1.8 convert_element_type.67
  106.2 2.1 copy.45
  108.4 0.6 convert_reduce_fusion.1
  109.0 51.2 %all-reduce.5.cloned.1.call-done = bf16[128,32,32]{0,2,1:T(8,128)(2,1)} async-done(((bf16[128,32,32]{0,2,1:T(8,128)(2,1)}), bf16[128,32,32]{0,2,1:T(8,128)(2,1)}) %all-reduce.5.cloned.1.call-update) | async-done | bytes 262160 | tf_op jit(solution)/shard_map/psum | solution.py:114
  160.2 1.6 fusion.28
  161.8 21.9 %reduce-scatter.4.cloned.1.call-done = bf16[32,16,32]{2,1,0:T(8,128)(2,1)} async-done(((bf16[128,16,32]{2,1,0:T(8,128)(2,1)}), bf16[32,16,32]{2,1,0:T(8,128)(2,1)}) %reduce-scatter.4.cloned.1.call-update) | async-done | bytes 32784 | tf_op jit(solution)/shard_map/reduce_scatter | solution.py:111
  183.7 1.1 fusion.29
  184.8 1.7 convolution_bitcast_fusion.3
  186.5 32.9 %all-reduce.7.cloned.1.call-done = bf16[128,16,32]{0,2,1:T(8,128)(2,1)} async-done(((bf16[128,16,32]{0,2,1:T(8,128)(2,1)}), bf16[128,16,32]{0,2,1:T(8,128)(2,1)}) %all-reduce.7.cloned.1.call-update) | async-done | bytes 131088 | tf_op jit(solution)/shard_map/psum | solution.py:9
  219.4 1.0 convert_convert_fusion
  220.4 0.2 copy.46
  220.6 0.8 convolution_bitcast_fusion.2
  221.4 0.3 multiply_reduce_fusion
  221.7 0.8 fusion.26
  222.6 0.7 convert_element_type.73
  223.4 0.1 div.63
  223.5 1.0 fusion.25
  224.5 122.1 %all-reduce.9.cloned.1.call-done = (f32[256,32]{0,1:T(8,128)}, f32[256,32]{0,1:T(8,128)}, f32[256]{0:T(256)}, f32[128]{0:T(128)}) async-done(((f32[256,32]{0,1:T(8,128)}, f32[256,32]{0,1:T(8,128)}, f32[256]{0:T(256)}, f32[128]{0:T(128)}), (f32[256,32]{0,1:T(8,128)}, f32[256,32]{0,1:T(8,128)}, f32[256]{0:T(256)}, f32[128]{0:T(128)})) %all-reduce.9.cloned.1.call-update) | async-done | bytes 67088 | tf_op jit(solution)/shard_map/psum | solution.py:155
  346.7 1.2 broadcast_multiply_fusion.6
  347.9 1.4 broadcast_multiply_fusion
  349.3 37.1 %reduce-scatter.6.cloned.1.call-done = bf16[128,128]{1,0:T(8,128)(2,1)} async-done(((bf16[1024,128]{1,0:T(8,128)(2,1)}), bf16[128,128]{1,0:T(8,128)(2,1)}) %reduce-scatter.6.cloned.1.call-update) | async-done | bytes 32784 | tf_op jit(solution)/shard_map/reduce_scatter | solution.py:156
  386.4 1.4 convert_element_type.74
  387.8 1.1 broadcast_multiply_fusion.7
  388.9 19.1 %reduce-scatter.8.cloned.1.call-done = f32[32,128]{1,0:T(8,128)} async-done(((f32[128,128]{1,0:T(8,128)}), f32[32,128]{1,0:T(8,128)}) %reduce-scatter.8.cloned.1.call-update) | async-done | bytes 16400 | tf_op jit(solution)/shard_map/reduce_scatter | solution.py:159
  408.0 1.3 broadcast_multiply_fusion.2
  (66 shorter events, 0.6 us)
Async XLA Ops:
  7.2 3.6 copy-start
  7.2 22.1 %copy-start.12 = (bf16[256,32]{0,1:T(8,128)(2,1)S(1)}, bf16[256,32]{0,1:T(8,128)(2,1)}, u32[]{:S(2)}) copy-start(bf16[256,32]{0,1:T(8,128)(2,1)} %param.11) | copy-start | bytes 49156
  7.2 61.3 %all-gather.2.cloned.1.call-start = ((), (), s32[]{:S(2)}) async-start(), calls=%async_computation.3 | async-start | bytes 4718592 | tf_op jit(solution)/shard_map/all_gather | solution.py:56
  8.3 2.4 copy-start.8
  9.6 1.2 copy-start.10
  10.8 18.8 %copy-start.5 = (bf16[32,16,256]{2,1,0:T(8,128)(2,1)}, bf16[32,16,256]{2,1,0:T(8,128)(2,1)S(1)}, u32[]{:S(2)}) copy-start(bf16[32,16,256]{2,1,0:T(8,128)(2,1)S(1)} %fusion.21) | copy-start | bytes 786436
  29.1 131.0 %all-reduce.5.cloned.1.call-start = ((), (), s32[]{:S(2)}) async-start(), calls=%async_computation.5 | async-start | bytes 524288 | tf_op jit(solution)/shard_map/psum | solution.py:114
  45.9 25.7 %copy-start.1 = (bf16[1024,128]{1,0:T(8,128)(2,1)S(1)}, bf16[1024,128]{1,0:T(8,128)(2,1)}, u32[]{:S(2)}) copy-start(bf16[1024,128]{1,0:T(8,128)(2,1)} %param.13) | copy-start | bytes 786436
  80.0 0.8 copy-start.2
  82.7 1.6 copy-start.15
  82.7 1.9 copy-start.16
  84.3 3.1 copy-start.3
  84.6 0.7 copy-start.17
  95.8 0.8 copy-start.2
  98.5 2.7 copy-start.15
  98.5 2.9 copy-start.16
  101.1 3.1 copy-start.3
  101.5 0.7 copy-start.17
  104.2 4.1 copy-start.7
  104.2 79.5 %copy-start.13 = (bf16[256,32]{0,1:T(8,128)(2,1)S(1)}, bf16[256,32]{0,1:T(8,128)(2,1)}, u32[]{:S(2)}) copy-start(bf16[256,32]{0,1:T(8,128)(2,1)} %param.11) | copy-start | bytes 49156
  104.2 80.6 %copy-start.6 = (bf16[32,16,256]{2,1,0:T(8,128)(2,1)S(1)}, bf16[32,16,256]{2,1,0:T(8,128)(2,1)}, u32[]{:S(2)}) copy-start(bf16[32,16,256]{2,1,0:T(8,128)(2,1)} %copy-done.5) | copy-start | bytes 786436
  106.1 115.3 %copy-start.14 = (f32[256]{0:T(256)S(1)}, f32[256]{0:T(256)}, u32[]{:S(2)}) copy-start(f32[256]{0:T(256)} %param.10) | copy-start | bytes 3076
  106.1 77.6 %reduce-scatter.4.cloned.1.call-start = ((), (), s32[]{:S(2)}) async-start(), calls=%async_computation.4 | async-start | bytes 655360 | tf_op jit(solution)/shard_map/reduce_scatter | solution.py:111
  108.3 113.5 %copy-start.4 = (bf16[32,16,256]{2,1,0:T(8,128)(2,1)S(1)}, bf16[32,16,256]{2,1,0:T(8,128)(2,1)}, u32[]{:S(2)}) copy-start(bf16[32,16,256]{2,1,0:T(8,128)(2,1)} %param.9) | copy-start | bytes 786436
  108.3 113.5 %copy-start.9 = (f32[32,16]{1,0:T(8,128)S(1)}, f32[32,16]{1,0:T(8,128)}, u32[]{:S(2)}) copy-start(f32[32,16]{1,0:T(8,128)} %copy-done.8) | copy-start | bytes 6148
  108.3 113.5 %copy-start.11 = (f32[32,16]{1,0:T(8,128)S(1)}, f32[32,16]{1,0:T(8,128)}, u32[]{:S(2)}) copy-start(f32[32,16]{1,0:T(8,128)} %copy-done.10) | copy-start | bytes 6148
  108.3 111.1 %all-reduce.7.cloned.1.call-start = ((), (), s32[]{:S(2)}) async-start(), calls=%async_computation.6 | async-start | bytes 262144 | tf_op jit(solution)/shard_map/psum | solution.py:9
  161.8 184.9 %all-reduce.9.cloned.1.call-start = ((), (), s32[]{:S(2)}) async-start(), calls=%async_computation.9 | async-start | bytes 134144 | tf_op jit(solution)/shard_map/psum | solution.py:155
  222.5 163.9 %reduce-scatter.6.cloned.1.call-start = ((), (), s32[]{:S(2)}) async-start(), calls=%async_computation.7 | async-start | bytes 294912 | tf_op jit(solution)/shard_map/reduce_scatter | solution.py:156
  223.3 184.6 %reduce-scatter.8.cloned.1.call-start = ((), (), s32[]{:S(2)}) async-start(), calls=%async_computation.8 | async-start | bytes 81920 | tf_op jit(solution)/shard_map/reduce_scatter | solution.py:159
Sparse Core Ops, SparseCore 0:
  29.3 39.2 all-gather.1
  106.2 53.8 all-reduce.4
  162.4 21.2 reduce-scatter.3
  186.5 32.8 all-reduce.6
  225.9 120.6 all-reduce.8
  349.5 36.8 reduce-scatter.5
  388.6 19.2 reduce-scatter.7
where the time goes:
time: 417 us; the launch traced here: 416 us
  waiting for transfers between devices  306 us (73%)
  blocking collectives  34.3 us (8%)
  local copies, waits for them, and re-layouts  21 us (5%)
  matrix products  18.1 us (4%)
  other arithmetic  18 us (4%)
  between operations  14.4 us (3%)
    psum x1, waiting for transfers between devices, on_device(): lax.psum((weight_left, weight_right, gain_part, bias_part), ('row', 'col'))  122 us
    psum x1, waiting for transfers between devices, on_device(): lax.psum(right_acc.astype(jnp.bfloat16), 'row').astype(jnp.float32)  51.2 us
    reduce_scatter x1, waiting for transfers between devices, on_device(): lax.psum_scatter(projection_running_sum.astype(jnp.bfloat16), 'row', scat...  37.1 us
    psum x1, waiting for transfers between devices, from_root(): return lax.psum(block, axis)  32.9 us
    reduce_scatter x1, waiting for transfers between devices, on_device(): lax.psum_scatter(left_partial.astype(jnp.bfloat16), 'col', scatter_dimens...  21.9 us
    all_gather x1, waiting for transfers between devices, on_device(): right_every = lax.all_gather(right_rows, 'row', axis=1, tiled=True)  21.7 us
    reduce_scatter x1, waiting for transfers between devices, on_device(): lax.psum_scatter(proj_partial, 'col', scatter_dimension=0, tiled=True)  19.1 us
    all_gather x1, blocking collectives, on_device(): lax.all_gather(right_local, 'col', axis=0, tiled=True)  18 us
  transfers between devices with their start and end apart: 7, of which 7 were waited for; matrix products, arithmetic and copies ran while one was open for 3% of the time, Pallas kernels for 0%

commit v1 on v0

--- a/solution.py
+++ b/solution.py
@@ -152,7 +152,9 @@
     )
     gain_part = jnp.sum(normed_derivative * normed_alignment, axis=(0, 1))
     bias_part = jnp.sum(pair_update_cotangent, axis=(0, 1), dtype=jnp.float32)
-    param_totals = lax.psum((weight_left, weight_right, gain_part, bias_part), ("row", "col"))
+    param_totals = jax.lax.psum(
+        jax.lax.psum((weight_left, weight_right, gain_part, bias_part), "row"), "col"
+    )
     proj_partial = lax.psum_scatter(
         projection_running_sum.astype(jnp.bfloat16), "row", scatter_dimension=0, tiled=True
     ).astype(jnp.float32)

time: 417 us -> 379 us (0.909)
  waiting for transfers between devices: 306 us -> 268 us
    psum x1 -> x2, waiting for transfers between devices: 122 us -> 87.6 us  [the longest x1 51.4 us: on_device(): jax.lax.psum((weight_left, weight_right, gain_part, bias_part), 'row')]
  transfers between devices with their start and end apart: 7 -> 8, of which waited for: 7 -> 8; matrix products, arithmetic and copies ran while one was open for 3% -> 4% of each run, Pallas kernels for 0% -> 0%
where the time goes in v1:
time: 379 us
  waiting for transfers between devices  268 us (71%)
  blocking collectives  34.3 us (9%)
  local copies, waits for them, and re-layouts  20.9 us (6%)
  matrix products  18.1 us (5%)
  other arithmetic  18 us (5%)
  between operations  14.4 us (4%)
  loops' own time  4.07 us (1%)
    psum x1, waiting for transfers between devices, on_device(): jax.lax.psum((weight_left, weight_right, gain_part, bias_part), 'row')  51.4 us
    psum x1, waiting for transfers between devices, on_device(): lax.psum(right_acc.astype(jnp.bfloat16), 'row').astype(jnp.float32)  51.2 us
    psum x1, waiting for transfers between devices, on_device(): jax.lax.psum(jax.lax.psum((weight_left, weight_right, gain_part, bias_par...  36.1 us
    reduce_scatter x1, waiting for transfers between devices, on_device(): lax.psum_scatter(projection_running_sum.astype(jnp.bfloat16), 'row', scat...  34.1 us
    psum x1, waiting for transfers between devices, from_root(): return lax.psum(block, axis)  32.9 us
    reduce_scatter x1, waiting for transfers between devices, on_device(): lax.psum_scatter(left_partial.astype(jnp.bfloat16), 'col', scatter_dimens...  21.9 us
    all_gather x1, waiting for transfers between devices, on_device(): right_every = lax.all_gather(right_rows, 'row', axis=1, tiled=True)  21.7 us
    reduce_scatter x1, waiting for transfers between devices, on_device(): lax.psum_scatter(proj_partial, 'col', scatter_dimension=0, tiled=True)  19 us
  transfers between devices with their start and end apart: 8, of which 8 were waited for; matrix products, arithmetic and copies ran while one was open for 4% of the time, Pallas kernels for 0%

profile of v1, /device:TPU:0, one launch (start us, length us, event | category | flops | bytes accessed | tf_op | source)
XLA Modules:
  0.0 378.6 jit_solution(17549846217125612770)
XLA Ops:
  7.2 1.1 convert_reduce_fusion
  8.4 1.2 fusion.27
  9.6 1.2 fusion.21
  10.8 0.2 convolution_convert_fusion.1
  11.0 0.1 copy.42
  11.1 18.0 %all_gather.10 = bf16[128,16,32]{2,1,0:T(8,128)(2,1)} all-gather(bf16[32,16,32]{2,1,0:T(8,128)(2,1)S(1)} %bitcast.126), channel_id=1, replica_groups=mesh['row'=8,'col'=4] {'col'}, dimensions={0}, use_global_device_ids=true | all-gather | bytes 163840 | tf_op jit(solution)/shard_map/all_gather | solution.py:53
  29.2 0.2 convolution_convert_fusion.2
  29.4 0.1 copy.41
  29.6 16.3 %all_gather.9 = bf16[128,16,32]{2,1,0:T(8,128)(2,1)S(1)} all-gather(bf16[32,16,32]{2,1,0:T(8,128)(2,1)S(1)} %bitcast.127), channel_id=1, replica_groups=mesh['row'=8,'col'=4] {'col'}, dimensions={0}, use_global_device_ids=true | all-gather | bytes 163840 | tf_op jit(solution)/shard_map/all_gather | solution.py:52
  45.9 0.4 copy.43
  46.3 0.5 iota_multiply_fusion
  46.8 21.7 %all-gather.2.cloned.1.call-done = bf16[128,128,32]{2,1,0:T(8,128)(2,1)} async-done(((bf16[128,16,32]{2,1,0:T(8,128)(2,1)}), bf16[128,128,32]{2,1,0:T(8,128)(2,1)}) %all-gather.2.cloned.1.call-update) | async-done | bytes 1048592 | tf_op jit(solution)/shard_map/all_gather | solution.py:56
  68.5 1.3 constant_dynamic-slice_fusion.1
  69.8 1.8 copy.44
  71.6 32.6 %while.17 = (s32[]{:T(128)}, f32[128,32,32]{0,2,1:T(8,128)}, f32[1024,128]{1,0:T(8,128)S(1)}, bf16[2,8,32,128]{3,2,1,0:T(8,128)(2,1)}, bf16[2,128,8,32]{1,3,2,0:...) while((s32[]{:T(128)}, f32[128,32,32]{0,2,1:T(8,128)}, ...), condition=%wide.region_3.4_spmd.clone, body=%wide.region_2.3_spmd.clone.sunk | while | flops 404193280 | bytes 15928666 | solution.py:106
  71.6 1.2 dynamic_slice.46
  74.8 1.7 fusion.79
  76.5 2.2 reshape.95
  78.7 0.9 constant_dynamic-slice_fusion.3
  79.5 0.5 convolution_add_fusion.4
  80.0 0.8 copy-done.2
  80.8 0.3 convolution_convert_fusion.4
  81.1 1.6 reshape.94
  82.7 1.5 fusion.78
  84.3 0.3 fusion.80
  84.6 0.6 copy-done.17
  85.2 2.1 fusion.81
  87.4 1.2 dynamic_slice.46
  90.6 1.7 fusion.79
  92.2 2.2 reshape.95
  94.5 0.9 constant_dynamic-slice_fusion.3
  95.3 0.5 convolution_add_fusion.4
  95.8 0.8 copy-done.2
  96.6 0.3 convolution_convert_fusion.4
  96.9 1.6 reshape.94
  98.5 2.6 fusion.78
  101.1 0.3 fusion.80
  101.4 0.6 copy-done.17
  102.1 2.1 fusion.81
  104.2 1.8 convert_element_type.67
  106.1 2.1 copy.45
  108.3 0.6 convert_reduce_fusion.1
  108.9 51.2 %all-reduce.7.cloned.1.call-done = bf16[128,32,32]{0,2,1:T(8,128)(2,1)} async-done(((bf16[128,32,32]{0,2,1:T(8,128)(2,1)}), bf16[128,32,32]{0,2,1:T(8,128)(2,1)}) %all-reduce.7.cloned.1.call-update) | async-done | bytes 262160 | tf_op jit(solution)/shard_map/psum | solution.py:114
  160.1 1.6 fusion.28
  161.8 21.9 %reduce-scatter.4.cloned.1.call-done = bf16[32,16,32]{2,1,0:T(8,128)(2,1)} async-done(((bf16[128,16,32]{2,1,0:T(8,128)(2,1)}), bf16[32,16,32]{2,1,0:T(8,128)(2,1)}) %reduce-scatter.4.cloned.1.call-update) | async-done | bytes 32784 | tf_op jit(solution)/shard_map/reduce_scatter | solution.py:111
  183.7 1.1 fusion.29
  184.8 1.7 convolution_bitcast_fusion.3
  186.5 32.9 %all-reduce.9.cloned.1.call-done = bf16[128,16,32]{0,2,1:T(8,128)(2,1)} async-done(((bf16[128,16,32]{0,2,1:T(8,128)(2,1)}), bf16[128,16,32]{0,2,1:T(8,128)(2,1)}) %all-reduce.9.cloned.1.call-update) | async-done | bytes 131088 | tf_op jit(solution)/shard_map/psum | solution.py:9
  219.4 1.0 convert_convert_fusion
  220.4 0.2 copy.46
  220.5 0.8 convolution_bitcast_fusion.2
  221.4 0.3 multiply_reduce_fusion
  221.7 0.8 fusion.26
  222.5 51.4 %all-reduce.11.cloned.1.call-done = (f32[256,32]{0,1:T(8,128)}, f32[256,32]{0,1:T(8,128)}, f32[256]{0:T(256)}, f32[128]{0:T(128)}) async-done(((f32[256,32]{0,1:T(8,128)}, f32[256,32]{0,1:T(8,128)}, f32[256]{0:T(256)}, f32[128]{0:T(128)}), (f32[256,32]{0,1:T(8,128)}, f32[256,32]{0,1:T(8,128)}, f32[256]{0:T(256)}, f32[128]{0:T(128)})) %all-reduce.11.cloned.1.call-update) | async-done | bytes 67088 | tf_op jit(solution)/shard_map/psum | solution.py:156
  274.0 0.7 convert_element_type.73
  274.9 1.0 fusion.25
  276.0 36.1 %all-reduce.13.cloned.1.call-done = (f32[256,32]{0,1:T(8,128)}, f32[256,32]{0,1:T(8,128)}, f32[256]{0:T(256)}, f32[128]{0:T(128)}) async-done(((f32[256,32]{0,1:T(8,128)}, f32[256,32]{0,1:T(8,128)}, f32[256]{0:T(256)}, f32[128]{0:T(128)}), (f32[256,32]{0,1:T(8,128)}, f32[256,32]{0,1:T(8,128)}, f32[256]{0:T(256)}, f32[128]{0:T(128)})) %all-reduce.13.cloned.1.call-update) | async-done | bytes 67088 | tf_op jit(solution)/shard_map/psum | solution.py:155
  312.1 1.2 broadcast_multiply_fusion.6
  313.4 1.4 broadcast_multiply_fusion
  314.8 34.1 %reduce-scatter.6.cloned.1.call-done = bf16[128,128]{1,0:T(8,128)(2,1)} async-done(((bf16[1024,128]{1,0:T(8,128)(2,1)}), bf16[128,128]{1,0:T(8,128)(2,1)}) %reduce-scatter.6.cloned.1.call-update) | async-done | bytes 32784 | tf_op jit(solution)/shard_map/reduce_scatter | solution.py:158
  348.9 1.4 convert_element_type.74
  350.3 1.1 broadcast_multiply_fusion.7
  351.4 19.0 %reduce-scatter.8.cloned.1.call-done = f32[32,128]{1,0:T(8,128)} async-done(((f32[128,128]{1,0:T(8,128)}), f32[32,128]{1,0:T(8,128)}) %reduce-scatter.8.cloned.1.call-update) | async-done | bytes 16400 | tf_op jit(solution)/shard_map/reduce_scatter | solution.py:161
  370.4 1.3 broadcast_multiply_fusion.2
  (69 shorter events, 0.7 us)
Async XLA Ops:
  7.2 3.6 copy-start
  7.2 22.1 %copy-start.12 = (bf16[256,32]{0,1:T(8,128)(2,1)S(1)}, bf16[256,32]{0,1:T(8,128)(2,1)}, u32[]{:S(2)}) copy-start(bf16[256,32]{0,1:T(8,128)(2,1)} %param.11) | copy-start | bytes 49156
  7.2 61.3 %all-gather.2.cloned.1.call-start = ((), (), s32[]{:S(2)}) async-start(), calls=%async_computation.3 | async-start | bytes 4718592 | tf_op jit(solution)/shard_map/all_gather | solution.py:56
  8.3 2.4 copy-start.8
  9.6 1.2 copy-start.10
  10.8 18.8 %copy-start.5 = (bf16[32,16,256]{2,1,0:T(8,128)(2,1)}, bf16[32,16,256]{2,1,0:T(8,128)(2,1)S(1)}, u32[]{:S(2)}) copy-start(bf16[32,16,256]{2,1,0:T(8,128)(2,1)S(1)} %fusion.21) | copy-start | bytes 786436
  29.1 131.0 %all-reduce.7.cloned.1.call-start = ((), (), s32[]{:S(2)}) async-start(), calls=%async_computation.5 | async-start | bytes 524288 | tf_op jit(solution)/shard_map/psum | solution.py:114
  45.9 25.7 %copy-start.1 = (bf16[1024,128]{1,0:T(8,128)(2,1)S(1)}, bf16[1024,128]{1,0:T(8,128)(2,1)}, u32[]{:S(2)}) copy-start(bf16[1024,128]{1,0:T(8,128)(2,1)} %param.13) | copy-start | bytes 786436
  80.0 0.8 copy-start.2
  82.7 1.6 copy-start.15
  82.7 1.8 copy-start.16
  84.3 3.1 copy-start.3
  84.6 0.7 copy-start.17
  95.8 0.8 copy-start.2
  98.5 2.6 copy-start.15
  98.5 2.9 copy-start.16
  101.1 3.1 copy-start.3
  101.4 0.7 copy-start.17
  104.2 4.1 %copy-start.7 = (bf16[16,32,128]{2,1,0:T(8,128)(2,1)S(1)}, bf16[16,32,128]{2,1,0:T(8,128)(2,1)}, u32[]{:S(2)}) copy-start(bf16[16,32,128]{2,1,0:T(8,128)(2,1)} %get-tuple-element.311) | copy-start | bytes 393220
  104.2 79.5 %copy-start.13 = (bf16[256,32]{0,1:T(8,128)(2,1)S(1)}, bf16[256,32]{0,1:T(8,128)(2,1)}, u32[]{:S(2)}) copy-start(bf16[256,32]{0,1:T(8,128)(2,1)} %param.11) | copy-start | bytes 49156
  104.2 80.6 %copy-start.6 = (bf16[32,16,256]{2,1,0:T(8,128)(2,1)S(1)}, bf16[32,16,256]{2,1,0:T(8,128)(2,1)}, u32[]{:S(2)}) copy-start(bf16[32,16,256]{2,1,0:T(8,128)(2,1)} %copy-done.5) | copy-start | bytes 786436
  106.1 115.3 %copy-start.14 = (f32[256]{0:T(256)S(1)}, f32[256]{0:T(256)}, u32[]{:S(2)}) copy-start(f32[256]{0:T(256)} %param.10) | copy-start | bytes 3076
  106.1 77.6 %reduce-scatter.4.cloned.1.call-start = ((), (), s32[]{:S(2)}) async-start(), calls=%async_computation.4 | async-start | bytes 655360 | tf_op jit(solution)/shard_map/reduce_scatter | solution.py:111
  108.2 113.4 %copy-start.4 = (bf16[32,16,256]{2,1,0:T(8,128)(2,1)S(1)}, bf16[32,16,256]{2,1,0:T(8,128)(2,1)}, u32[]{:S(2)}) copy-start(bf16[32,16,256]{2,1,0:T(8,128)(2,1)} %param.9) | copy-start | bytes 786436
  108.2 113.5 %copy-start.9 = (f32[32,16]{1,0:T(8,128)S(1)}, f32[32,16]{1,0:T(8,128)}, u32[]{:S(2)}) copy-start(f32[32,16]{1,0:T(8,128)} %copy-done.8) | copy-start | bytes 6148
  108.2 113.5 %copy-start.11 = (f32[32,16]{1,0:T(8,128)S(1)}, f32[32,16]{1,0:T(8,128)}, u32[]{:S(2)}) copy-start(f32[32,16]{1,0:T(8,128)} %copy-done.10) | copy-start | bytes 6148
  108.2 111.1 %all-reduce.9.cloned.1.call-start = ((), (), s32[]{:S(2)}) async-start(), calls=%async_computation.6 | async-start | bytes 262144 | tf_op jit(solution)/shard_map/psum | solution.py:9
  161.7 112.2 %all-reduce.11.cloned.1.call-start = ((), (), s32[]{:S(2)}) async-start(), calls=%async_computation.9 | async-start | bytes 134144 | tf_op jit(solution)/shard_map/psum | solution.py:156
  222.5 89.6 %all-reduce.13.cloned.1.call-start = ((), (), s32[]{:S(2)}) async-start(), calls=%async_computation.10 | async-start | bytes 134144 | tf_op jit(solution)/shard_map/psum | solution.py:155
  274.0 74.9 %reduce-scatter.6.cloned.1.call-start = ((), (), s32[]{:S(2)}) async-start(), calls=%async_computation.7 | async-start | bytes 294912 | tf_op jit(solution)/shard_map/reduce_scatter | solution.py:158
  274.8 95.6 %reduce-scatter.8.cloned.1.call-start = ((), (), s32[]{:S(2)}) async-start(), calls=%async_computation.8 | async-start | bytes 81920 | tf_op jit(solution)/shard_map/reduce_scatter | solution.py:161
Sparse Core Ops, SparseCore 0:
  29.3 39.2 all-gather.1
  106.2 53.8 all-reduce.6
  162.4 21.2 reduce-scatter.3
  186.4 32.8 all-reduce.8
  223.3 50.6 all-reduce.10
  276.4 35.6 all-reduce.12
  315.2 33.6 reduce-scatter.5
  351.1 19.2 reduce-scatter.7
